TPU v7x, 32 devices: a whole 2x2x4 slice. The times are simulated.
32 devices in a mesh: bucket: 4 (over y, x), seq: 8 (over z, core).
Axes of the slice: x: 2, y: 2, z: 4, core: 2. Of those that a mesh axis runs over, the one named last changes fastest.
Arguments:
- queries: bfloat16 [4, 448, 1536], P('bucket', 'seq'), may hold values from -45 to 45, as said below
- keys: bfloat16 [4, 448, 1536], P('bucket', 'seq'), may hold values from -5 to 5
- values: bfloat16 [4, 448, 1536], P('bucket', 'seq'), may hold values from -6 to 6
- bucket_lens: int32 [4], P('bucket'), may hold values from 224 to 392
- gate: float32 [4, 3072], P('bucket'), may hold values from 0.5 to 2
- out_weight: bfloat16 [1536, 3072], P(None, 'bucket'), may hold values from -0.15625 to 0.15625
Outputs:
- gated_out: bfloat16 [4, 448, 3072], P('bucket', 'seq')
Inputs may be any that keep to these rules, and one draw needn't show every extreme that they name: queries of a few tokens in a bucket may be strong multiples of some keys.
All inputs are finite; a program needn't handle non-finite values.
Results may differ from a plain program's by a relative error of at most 0.013.
Values may be sent and summed in bfloat16 or wider, within the bound.
No kernel may reach another device: no remote copies, remote signals or barrier semaphores. Data moves between devices by JAX's collectives and lax.ppermute only.
A program may use at most 192 MiB of HBM per device.

v0:
```python
import jax
import jax.numpy as jnp
from jax import lax
from jax.sharding import PartitionSpec as P

HEADS = 12
HEAD_DIM = 128


NEG_FILL = -1e30


def block_stats(queries, keys, values, usable):
    scores = jnp.einsum(
        "qhe,nkhe->nhqk", queries, keys, preferred_element_type=jnp.float32
    ) * HEAD_DIM ** (-0.5)
    keep_mask = usable[:, None, None, :]
    scores = jnp.where(keep_mask, scores, NEG_FILL)
    maxima = jnp.max(scores, axis=3)
    weights = jnp.where(keep_mask, jnp.exp(scores - maxima[..., None]), 0.0)
    totals = jnp.sum(weights, axis=3)
    weighted = jnp.einsum(
        "nhqk,nkhe->nqhe", weights.astype(jnp.bfloat16), values, preferred_element_type=jnp.float32
    )
    divisor = jnp.transpose(jnp.maximum(totals, 1.0), (0, 2, 1))
    partial_value = (weighted / divisor[..., None]).astype(jnp.bfloat16)
    return (partial_value, jnp.transpose(maxima, (0, 2, 1)), jnp.transpose(totals, (0, 2, 1)))


def combine(partial_value, maxima, totals):
    row_max = jnp.max(maxima, axis=0)
    factors = totals * jnp.exp(maxima - row_max[None])
    summed = jnp.einsum("nqh,nqhe->qhe", factors, partial_value.astype(jnp.float32))
    attended = summed / jnp.sum(factors, axis=0)[..., None]
    return attended.reshape(attended.shape[0], -1).astype(jnp.bfloat16)


def shards(queries, keys, values, bucket_lens, gate, out_weight):
    rows_here = queries.shape[1]
    width = queries.shape[2]
    length = bucket_lens[0]
    position = lax.axis_index("seq") * rows_here + lax.iota(jnp.int32, rows_here)
    queries_all = lax.all_gather(queries[0], "seq", axis=0, tiled=True)
    count_all = queries_all.shape[0]
    key_usable = (position < length)[None, :]
    partial_value, maxima, totals = block_stats(
        queries_all.reshape(count_all, HEADS, HEAD_DIM),
        keys[0].reshape(1, rows_here, HEADS, HEAD_DIM),
        values[0].reshape(1, rows_here, HEADS, HEAD_DIM),
        key_usable,
    )
    block_max, block_total = (
        lax.all_to_all(maxima, "seq", split_axis=1, concat_axis=0, tiled=True),
        lax.all_to_all(totals, "seq", split_axis=1, concat_axis=0, tiled=True),
    )
    block_part = lax.all_to_all(
        partial_value.reshape(1, count_all, width), "seq", split_axis=1, concat_axis=0, tiled=True
    )
    shaped = block_part.reshape(block_part.shape[0], block_part.shape[1], HEADS, HEAD_DIM)
    attended = combine(shaped, block_max, block_total)
    gate_row = gate[0]
    projected = (
        jnp.dot(
            attended,
            lax.all_gather(out_weight, "bucket", axis=1, tiled=True),
            preferred_element_type=jnp.float32,
        )
        * gate_row[None, :]
    )
    result = jnp.where((position < length)[:, None], projected, 0.0).astype(jnp.bfloat16)
    return result[None]


def solution(mesh):
    placed = (
        P("bucket", "seq", None),
        P("bucket", "seq", None),
        P("bucket", "seq", None),
        P("bucket"),
        P("bucket", None),
        P(None, "bucket"),
    )
    return jax.shard_map(
        shards, mesh=mesh, in_specs=placed, out_specs=P("bucket", "seq", None), check_vma=False
    )
```

profile of v0, /device:TPU:0, one launch (start us, length us, event | category | flops | bytes accessed | tf_op | source)
XLA Modules:
  0.0 148.8 jit_solution(12838060443762022646)
XLA Ops:
  6.5 0.7 all-gather.6.cloned.1.call-update
  7.3 0.7 all-gather.4.cloned.1.call-update
  9.0 26.6 %all-gather.6.cloned.1.call-done = bf16[1,448,1536]{2,1,0:T(8,128)(2,1)} async-done(((bf16[1,56,1536]{2,1,0:T(8,128)(2,1)}), bf16[1,448,1536]{2,1,0:T(8,128)(2,1)}) %all-gather.6.cloned.1.call-update) | async-done | bytes 1376272 | tf_op jit(solution)/shard_map/all_gather | solution.py:43
  35.6 1.7 %copy.26 = bf16[1,448,1536]{1,2,0:T(8,128)(2,1)S(1)} copy(bf16[1,448,1536]{2,1,0:T(8,128)(2,1)} %all-gather.6.cloned.1.call-done) | data formatting | bytes 2752512 | tf_op jit(solution)/shard_map/all_gather | solution.py:43
  37.3 0.4 bitcast_reduce_fusion
  37.7 0.3 fusion.11
  38.2 0.6 broadcast.44
  38.8 1.2 reduce.4
  40.0 0.8 reshape.81
  40.7 3.4 %all-to-all-start = ((f32[8,1,672]{2,1,0:T(1,128)}), f32[8,1,672]{2,1,0:T(1,128)S(1)}, u32[]{:S(2)}, u32[]{:S(2)}) async-start(f32[8,1,672]{2,1,0:T(1,128)} %reshape.81), calls=%async_computation | async-start | bytes 49152 | tf_op jit(solution)/shard_map/all_to_all | solution.py:54
  44.3 1.2 reduce.6
  45.5 0.8 reshape.83
  46.2 3.6 %all-to-all-done = f32[8,1,672]{2,1,0:T(1,128)S(1)} async-done(((f32[8,1,672]{2,1,0:T(1,128)}), f32[8,1,672]{2,1,0:T(1,128)S(1)}, u32[]{:S(2)}, u32[]{:S(2)}) %all-to-all-start) | async-done | bytes 21536 | tf_op jit(solution)/shard_map/all_to_all | solution.py:54
  49.8 3.5 %all-to-all-start.1 = ((f32[8,1,672]{2,1,0:T(1,128)}), f32[8,1,672]{2,1,0:T(1,128)S(1)}, u32[]{:S(2)}, u32[]{:S(2)}) async-start(f32[8,1,672]{2,1,0:T(1,128)} %reshape.83), calls=%async_computation.1 | async-start | bytes 49152 | tf_op jit(solution)/shard_map/all_to_all | solution.py:53
  53.3 1.5 fusion.3
  54.8 1.6 %copy.34 = bf16[1,448,12,128]{1,3,2,0:T(8,128)(2,1)} copy(bf16[1,448,12,128]{3,1,2,0:T(8,128)(2,1)S(1)} %fusion.3) | data formatting | bytes 2752512 | tf_op jit(solution)/shard_map/convert_element_type | solution.py:26
  56.4 7.6 %copy.35 = bf16[1,448,1536]{2,0,1:T(2,128)(2,1)S(1)} copy(bf16[1,448,1536]{1,2,0:T(8,128)(2,1)} %bitcast.72) | data formatting | bytes 2752512 | tf_op jit(solution)/shard_map/reshape | solution.py:57
  64.0 0.5 broadcast.48
  64.5 10.1 %reduce.8 = bf16[448,1536]{1,0:T(8,128)(2,1)} reduce(bf16[448,1,1536]{2,1,0:T(2,128)(2,1)S(1)} %bitcast.71, bf16[]{:T(256)} %broadcast.48), dimensions={1}, to_apply=%bitcast.64.reduce_sub_computation | reduce | bytes 2752514
  74.6 4.6 %reshape.85 = bf16[8,2,43008]{2,1,0:T(2,128)(2,1)} reshape(bf16[448,1536]{1,0:T(8,128)(2,1)} %reduce.8) | data formatting | bytes 2752512
  79.2 4.8 %all-to-all-start.2 = ((bf16[8,2,43008]{2,1,0:T(2,128)(2,1)}), bf16[8,2,43008]{2,1,0:T(2,128)(2,1)}, u32[]{:S(2)}, u32[]{:S(2)}) async-start(bf16[8,2,43008]{2,1,0:T(2,128)(2,1)} %reshape.85), calls=%async_computation.2 | async-start | bytes 2752512 | tf_op jit(solution)/shard_map/all_to_all | solution.py:56
  84.0 0.7 reduce.5
  84.7 0.4 reshape.82
  85.2 0.7 reduce.7
  85.9 0.4 reshape.84
  86.6 0.2 copy.38
  86.9 30.8 %all-to-all-done.2 = bf16[8,2,43008]{2,1,0:T(2,128)(2,1)} async-done(((bf16[8,2,43008]{2,1,0:T(2,128)(2,1)}), bf16[8,2,43008]{2,1,0:T(2,128)(2,1)}, u32[]{:S(2)}, u32[]{:S(2)}) %all-to-all-start.2) | async-done | bytes 1376288 | tf_op jit(solution)/shard_map/all_to_all | solution.py:56
  117.7 4.5 %reshape.86 = bf16[448,1,1536]{2,1,0:T(2,128)(2,1)S(1)} reshape(bf16[8,2,43008]{2,1,0:T(2,128)(2,1)} %all-to-all-done.2) | data formatting | bytes 2752512
  122.2 9.2 %bitcast_reduce_fusion.1 = bf16[448,1536]{1,0:T(8,128)(2,1)} fusion(bf16[448,1,1536]{2,1,0:T(2,128)(2,1)S(1)} %reshape.86), kind=kLoop, calls=%fused_computation.34 | loop fusion | bytes 2752512 | tf_op jit(solution)/shard_map/all_to_all | solution.py:56
  131.5 3.0 %reshape.75 = bf16[8,56,12,128]{3,2,1,0:T(8,128)(2,1)S(1)} reshape(bf16[448,1536]{1,0:T(8,128)(2,1)} %bitcast_reduce_fusion.1) | data formatting | bytes 2752512 | tf_op jit(solution)/shard_map/reshape | solution.py:59
  134.5 1.2 fusion.7
  135.9 6.1 %fusion.2 = bf16[1,56,3072]{2,1,0:T(8,128)(2,1)} fusion(bf16[1536,3072]{1,0:T(8,128)(2,1)} %all-gather.4.cloned.1.call-done, f32[3072]{0:T(1024)S(1)} %bitcast.82, pred[56]{0:T(512)(128)(4,1)S(1)} %add_compare_fusion, bf16[7,8,12,128]{3,2,1,0:T(8,128)(2,1)S(1)} %bitcast.76), kind=kOutput, calls=%fused_computation.3 | convolution fusion | flops 528998400 | bytes 9965624 | tf_op jit(solution)/shard_map/dot_general | solution.py:63
  (24 shorter events, 1.3 us)
Async XLA Ops:
  6.5 2.1 %copy-start = (bf16[1,56,1536]{2,1,0:T(8,128)(2,1)S(1)}, bf16[1,56,1536]{2,1,0:T(8,128)(2,1)}, u32[]{:S(2)}) copy-start(bf16[1,56,1536]{2,1,0:T(8,128)(2,1)} %param.7) | copy-start | bytes 516100
  6.5 29.0 %all-gather.6.cloned.1.call-start = ((), (), s32[]{:S(2)}) async-start(), calls=%async_computation.4 | async-start | bytes 1548288 | tf_op jit(solution)/shard_map/all_gather | solution.py:43
  7.3 1.6 %copy-start.1 = (bf16[1,56,1536]{2,1,0:T(8,128)(2,1)S(1)}, bf16[1,56,1536]{2,1,0:T(8,128)(2,1)}, u32[]{:S(2)}) copy-start(bf16[1,56,1536]{2,1,0:T(8,128)(2,1)} %param.8) | copy-start | bytes 516100
  7.3 128.6 %all-gather.4.cloned.1.call-start = ((), (), s32[]{:S(2)}) async-start(), calls=%async_computation.3 | async-start | bytes 11796480 | tf_op jit(solution)/shard_map/all_gather | solution.py:65
  40.7 9.0 %all-to-all-start = ((f32[8,1,672]{2,1,0:T(1,128)}), f32[8,1,672]{2,1,0:T(1,128)S(1)}, u32[]{:S(2)}, u32[]{:S(2)}) async-start(f32[8,1,672]{2,1,0:T(1,128)} %reshape.81), calls=%async_computation | async-start | bytes 49152 | tf_op jit(solution)/shard_map/all_to_all | solution.py:54
  49.8 29.4 %all-to-all-start.1 = ((f32[8,1,672]{2,1,0:T(1,128)}), f32[8,1,672]{2,1,0:T(1,128)S(1)}, u32[]{:S(2)}, u32[]{:S(2)}) async-start(f32[8,1,672]{2,1,0:T(1,128)} %reshape.83), calls=%async_computation.1 | async-start | bytes 49152 | tf_op jit(solution)/shard_map/all_to_all | solution.py:53
  79.2 38.5 %all-to-all-start.2 = ((bf16[8,2,43008]{2,1,0:T(2,128)(2,1)}), bf16[8,2,43008]{2,1,0:T(2,128)(2,1)}, u32[]{:S(2)}, u32[]{:S(2)}) async-start(bf16[8,2,43008]{2,1,0:T(2,128)(2,1)} %reshape.85), calls=%async_computation.2 | async-start | bytes 2752512 | tf_op jit(solution)/shard_map/all_to_all | solution.py:56
  134.5 1.4 copy-start.2
Sparse Core Ops, SparseCore 0:
  9.0 26.5 all-gather.5
  37.4 95.8 all-gather.3
where the time goes:
time: 150 us; the launch traced here: 149 us
  waiting for transfers between devices  62.4 us (42%)
  local copies, waits for them, and re-layouts  36.7 us (24%)
  other arithmetic  14.5 us (10%)
  between operations  14.3 us (10%)
  starting transfers between devices  11.7 us (8%)
  matrix products  9.18 us (6%)
    all_to_all x1, waiting for transfers between devices, shards(): lax.all_to_all(partial_value.reshape(1, count_all, width), 'seq', split_a...  30.8 us
    all_gather x1, waiting for transfers between devices, shards(): queries_all = lax.all_gather(queries[0], 'seq', axis=0, tiled=True)  26.6 us
    unnamed x15, local copies, waits for them, and re-layouts  12.6 us
    unnamed x3, other arithmetic  12.5 us
    all_to_all x1, local copies, waits for them, and re-layouts, shards(): lax.all_to_all(partial_value.reshape(1, count_all, width), 'seq', split_a...  9.25 us
    reshape x1, local copies, waits for them, and re-layouts, shards(): partial_value.reshape(1, count_all, width)  7.59 us
    dot_general x1, matrix products, shards(): jnp.dot(attended, lax.all_gather(out_weight, 'bucket', axis=1, tiled=True...  6.12 us
    all_to_all x1, starting transfers between devices, shards(): lax.all_to_all(partial_value.reshape(1, count_all, width), 'seq', split_a...  4.82 us
  transfers between devices with their start and end apart: 5, of which 3 were waited for; matrix products, arithmetic and copies ran while one was open for 36% of the time, Pallas kernels for 0%

commit v1 on v0

v1 whole, which is shorter than its diff:
```python
import jax
import jax.numpy as jnp
from jax import lax
from jax.sharding import PartitionSpec as P

HEADS = 12
HEAD_DIM = 128
NEG_FILL = -1e30
ROW_LIMIT = 512


def head_windows(parts):
    share = HEADS * HEAD_DIM // parts
    first = [(share * d) // HEAD_DIM for d in range(parts)]
    last = [-(-share * (d + 1) // HEAD_DIM) for d in range(parts)]
    slots = max(b - a for a, b in zip(first, last))
    return [min(a, HEADS - slots) for a in first], slots


def attend(query, key, value, usable):
    scores = lax.dot_general(
        query, key, (((1,), (1,)), ((), ())), preferred_element_type=jnp.float32
    ) * HEAD_DIM ** (-0.5)
    scores = jnp.where(usable, scores, NEG_FILL)
    weights = jnp.exp(scores - jnp.max(scores, axis=1, keepdims=True))
    total = jnp.sum(weights, axis=1, keepdims=True)
    out = jnp.dot(weights.astype(jnp.bfloat16), value, preferred_element_type=jnp.float32)
    return (out / total).astype(jnp.bfloat16)


def attend_rows(query, key, value, usable):
    rows = query.shape[0]
    if rows <= ROW_LIMIT:
        return attend(query, key, value, usable)
    steps = next(n for n in range(1, rows + 1) if rows % n == 0 and rows // n <= ROW_LIMIT)
    blocks = query.reshape(steps, rows // steps, query.shape[1])
    return lax.map(lambda block: attend(block, key, value, usable), blocks).reshape(query.shape)


def make_shards(parts):
    first, slots = head_windows(parts)
    wide = slots * HEAD_DIM

    def shards(queries, keys, values, bucket_lens, gate, out_weight):
        rows_here = queries.shape[1]
        length = bucket_lens[0]
        position = lax.axis_index("seq") * rows_here + lax.iota(jnp.int32, rows_here)
        pieces = []
        for start in first:
            cut = slice(start * HEAD_DIM, start * HEAD_DIM + wide)
            pieces.append(
                jnp.concatenate([queries[0][:, cut], keys[0][:, cut], values[0][:, cut]], axis=1)
            )
        mine = lax.all_to_all(jnp.stack(pieces), "seq", split_axis=0, concat_axis=0, tiled=True)
        count_all = parts * rows_here
        mine = mine.reshape(count_all, 3 * wide)
        usable = (lax.iota(jnp.int32, count_all) < length)[None, :]
        outs = []
        for slot in range(slots):
            q, k, v = (
                mine[:, which * wide + slot * HEAD_DIM : which * wide + (slot + 1) * HEAD_DIM]
                for which in range(3)
            )
            outs.append(attend_rows(q, k, v, usable))
        outs = jnp.concatenate(outs, axis=1).reshape(parts, rows_here, wide)
        back = lax.all_to_all(outs, "seq", split_axis=0, concat_axis=0, tiled=True)
        columns = []
        for head in range(HEADS):
            source = next(d for d in range(parts) if first[d] <= head < first[d] + slots)
            slot = head - first[source]
            columns.append(back[source][:, slot * HEAD_DIM : (slot + 1) * HEAD_DIM])
        attended = jnp.concatenate(columns, axis=1)
        everyone = lax.all_gather(attended, "bucket", axis=0, tiled=True)
        projected = jnp.dot(everyone, out_weight, preferred_element_type=jnp.float32)
        projected = projected.astype(jnp.bfloat16).reshape(-1, rows_here, out_weight.shape[1])
        gathered = lax.all_to_all(projected, "bucket", split_axis=0, concat_axis=0, tiled=True)
        wide_rows = jnp.concatenate([gathered[c] for c in range(gathered.shape[0])], axis=1)
        result = wide_rows.astype(jnp.float32) * gate[0][None, :]
        return jnp.where((position < length)[:, None], result, 0.0).astype(jnp.bfloat16)[None]

    return shards


def solution(mesh):
    placed = (
        P("bucket", "seq", None),
        P("bucket", "seq", None),
        P("bucket", "seq", None),
        P("bucket"),
        P("bucket", None),
        P(None, "bucket"),
    )
    return jax.shard_map(
        make_shards(mesh.shape["seq"]),
        mesh=mesh, in_specs=placed, out_specs=P("bucket", "seq", None), check_vma=False,
    )
```

time: 150 us -> 68.1 us (0.45)
  waiting for transfers between devices: 62.4 us -> 23.7 us
  local copies, waits for them, and re-layouts: 36.7 us -> 2.15 us
  blocking collectives: 0 us -> 22.1 us
  between operations: 14.3 us -> 0.78 us
  other arithmetic: 14.5 us -> 6.37 us
  matrix products: 9.18 us -> 2.79 us
  starting transfers between devices: 11.7 us -> 9.81 us
    all_gather x2 -> x0, waiting for transfers between devices: 26.6 us -> none  [the longest x1 26.6 us: shards(): queries_all = lax.all_gather(queries[0], 'seq', axis=0, tiled=True)]
    unnamed x15 -> x11, local copies, waits for them, and re-layouts: 12.6 us -> 0.06 us
    all_to_all x0 -> x1, blocking collectives: none -> 11.4 us  [shards(): back = lax.all_to_all(outs, 'seq', split_axis=0, concat_axis=0, tiled=True)]
    all_gather x0 -> x1, blocking collectives: none -> 10.7 us  [shards(): everyone = lax.all_gather(attended, 'bucket', axis=0, tiled=True)]
    all_to_all x3 -> x2, waiting for transfers between devices: 34.3 us -> 23.7 us  [the longest x1 18.2 us: shards(): lax.all_to_all(jnp.stack(pieces), 'seq', split_axis=0, concat_axis=0, til...]
    reshape x2 -> x0, local copies, waits for them, and re-layouts: 10.6 us -> none  [the longest x1 7.59 us: shards(): partial_value.reshape(1, count_all, width)]
    all_to_all x3 -> x0, local copies, waits for them, and re-layouts: 9.49 us -> none  [the longest x1 9.25 us: shards(): lax.all_to_all(partial_value.reshape(1, count_all, width), 'seq', split_a...]
    unnamed x3 -> x7, other arithmetic: 12.5 us -> 4.5 us
  transfers between devices with their start and end apart: 5 -> 2, of which waited for: 3 -> 2; matrix products, arithmetic and copies ran while one was open for 36% -> 0% of each run, Pallas kernels for 0% -> 0%
where the time goes in v1:
time: 68.1 us; the launch traced here: 67.8 us
  waiting for transfers between devices  23.7 us (35%)
  blocking collectives  22.1 us (32%)
  starting transfers between devices  9.81 us (14%)
  other arithmetic  6.37 us (9%)
  matrix products  2.79 us (4%)
  local copies, waits for them, and re-layouts  2.15 us (3%)
  between operations  0.78 us (1%)
    all_to_all x1, waiting for transfers between devices, shards(): lax.all_to_all(jnp.stack(pieces), 'seq', split_axis=0, concat_axis=0, til...  18.2 us
    all_to_all x1, blocking collectives, shards(): back = lax.all_to_all(outs, 'seq', split_axis=0, concat_axis=0, tiled=True)  11.4 us
    all_gather x1, blocking collectives, shards(): everyone = lax.all_gather(attended, 'bucket', axis=0, tiled=True)  10.7 us
    all_to_all x1, starting transfers between devices, shards(): lax.all_to_all(jnp.stack(pieces), 'seq', split_axis=0, concat_axis=0, til...  6.35 us
    all_to_all x1, waiting for transfers between devices, shards(): lax.all_to_all(projected, 'bucket', split_axis=0, concat_axis=0, tiled=True)  5.56 us
    unnamed x7, other arithmetic  4.5 us
    all_to_all x1, starting transfers between devices, shards(): lax.all_to_all(projected, 'bucket', split_axis=0, concat_axis=0, tiled=True)  3.46 us
    dot_general x1, matrix products, shards(): jnp.dot(everyone, out_weight, preferred_element_type=jnp.float32)  1.43 us
  transfers between devices with their start and end apart: 2, of which 2 were waited for; matrix products, arithmetic and copies ran while one was open for 0% of the time, Pallas kernels for 0%

profile of v1, /device:TPU:0, one launch (start us, length us, event | category | flops | bytes accessed | tf_op | source)
XLA Modules:
  0.0 67.8 jit_solution(12705393680919447636)
XLA Ops:
  0.0 0.0 copy-start
  0.0 1.0 %fusion.29 = (bf16[56,256]{1,0:T(8,128)(2,1)S(1)}, bf16[56,256]{1,0:T(8,128)(2,1)S(1)}, bf16[56,256]{1,0:T(8,128)(2,1)S(1)}, bf16[56,256]{1,0:T(8,128)(2,1)S(1)}...) fusion(bf16[56,1536]{1,0:T(8,128)(2,1)} %bitcast.75), kind=kLoop, calls=%fused_computation.62 | loop fusion | bytes 458752 | tf_op jit(solution)/shard_map/slice | solution.py:52
  1.0 1.0 %fusion.27 = (bf16[56,256]{1,0:T(8,128)(2,1)S(1)}, bf16[56,256]{1,0:T(8,128)(2,1)S(1)}, bf16[56,256]{1,0:T(8,128)(2,1)S(1)}, bf16[56,256]{1,0:T(8,128)(2,1)S(1)}...) fusion(bf16[56,1536]{1,0:T(8,128)(2,1)} %bitcast.73, ...), kind=kLoop, calls=%fused_computation.60 | loop fusion | bytes 917504 | tf_op jit(solution)/shard_map/slice | solution.py:52
  2.1 0.6 fusion.18
  2.7 0.6 fusion.19
  3.4 0.6 fusion.20
  4.0 0.6 fusion.21
  4.6 0.6 fusion.22
  5.3 0.6 fusion.23
  5.9 0.6 fusion.24
  6.6 0.6 fusion.25
  7.2 6.4 %all-to-all-start = ((bf16[8,56,768]{2,1,0:T(8,128)(2,1)}), bf16[8,56,768]{2,1,0:T(8,128)(2,1)S(1)}, u32[]{:S(2)}, u32[]{:S(2)}) async-start(bf16[8,56,768]{2,1,0:T(8,128)(2,1)} %fusion.25), calls=%async_computation | async-start | bytes 1376256 | tf_op jit(solution)/shard_map/all_to_all | solution.py:54
  14.2 18.2 %all-to-all-done = bf16[8,56,768]{2,1,0:T(8,128)(2,1)S(1)} async-done(((bf16[8,56,768]{2,1,0:T(8,128)(2,1)}), bf16[8,56,768]{2,1,0:T(8,128)(2,1)S(1)}, u32[]{:S(2)}, u32[]{:S(2)}) %all-to-all-start) | async-done | bytes 688160 | tf_op jit(solution)/shard_map/all_to_all | solution.py:54
  32.4 0.3 fusion.31
  32.7 0.3 fusion.30
  33.0 0.2 fusion.4
  33.2 0.4 fusion.2
  33.6 0.2 fusion.6
  33.8 0.4 fusion.3
  34.2 11.4 %all_to_all.15 = bf16[8,56,256]{2,1,0:T(8,128)(2,1)S(1)} all-to-all(bf16[8,56,256]{2,1,0:T(8,128)(2,1)S(1)} %bitcast.72), channel_id=1, replica_groups=mesh['bucket'=4,'seq'=8] {'seq'}, dimensions={0} | all-to-all | bytes 458752 | tf_op jit(solution)/shard_map/all_to_all | solution.py:66
  45.7 10.7 %all_gather.3 = bf16[224,1536]{1,0:T(8,128)(2,1)S(1)} all-gather(bf16[56,1536]{1,0:T(8,128)(2,1)S(1)} %constant_dynamic-update-slice_fusion), channel_id=1, replica_groups=mesh['bucket'=4,'seq'=8] {'bucket'}, dimensions={0}, use_global_device_ids=true | all-gather | bytes 860160 | tf_op jit(solution)/shard_map/all_gather | solution.py:73
  56.4 0.0 copy-done
  56.4 0.0 copy-start.1
  56.4 1.4 %convolution_convert_fusion = bf16[224,768]{1,0:T(8,128)(2,1)} fusion(bf16[224,1536]{1,0:T(8,128)(2,1)S(1)} %all_gather.3, bf16[1536,768]{1,0:T(8,128)(2,1)S(1)} %copy-done), kind=kOutput, calls=%fused_computation.4 | convolution fusion | flops 528654336 | bytes 3391488 | tf_op jit(solution)/shard_map/dot_general | solution.py:74
  57.8 3.5 %all-to-all-start.2 = ((bf16[4,56,768]{2,1,0:T(8,128)(2,1)}), bf16[4,56,768]{2,1,0:T(8,128)(2,1)S(1)}, u32[]{:S(2)}, u32[]{:S(2)}) async-start(bf16[4,56,768]{2,1,0:T(8,128)(2,1)} %bitcast.22), calls=%async_computation.2 | async-start | bytes 688128 | tf_op jit(solution)/shard_map/all_to_all | solution.py:76
  61.3 5.6 %all-to-all-done.2 = bf16[4,56,768]{2,1,0:T(8,128)(2,1)S(1)} async-done(((bf16[4,56,768]{2,1,0:T(8,128)(2,1)}), bf16[4,56,768]{2,1,0:T(8,128)(2,1)S(1)}, u32[]{:S(2)}, u32[]{:S(2)}) %all-to-all-start.2) | async-done | bytes 344096 | tf_op jit(solution)/shard_map/all_to_all | solution.py:76
  66.9 0.0 copy-done.1
  66.9 0.8 %select_convert_fusion = bf16[1,56,3072]{2,1,0:T(8,128)(2,1)} fusion(bf16[1,56,768]{2,1,0:T(8,128)(2,1)S(1)} %get-tuple-element.6, bf16[1,56,768]{2,1,0:T(8,128)(2,1)S(1)} %get-tuple-element.7, bf16[1,56,768]{2,1,0:T(8,128)(2,1)S(1)} %get-tuple-element.8, bf16[1,56,768]{2,1,0:T(8,128)(2,1)S(1)} %get-tuple-element.5, f32[3072]{0:T(1024)S(1)} %bitcast.76, ...), kind=kLoop, calls=%fused_computation.15 | loop fusion | flops 1892352 | bytes 700472 | tf_op jit(solution)/shard_map/convert_element_type | solution.py:79
  (13 shorter events, 0.1 us)
Async XLA Ops:
  0.0 56.4 %copy-start = (bf16[1536,768]{1,0:T(8,128)(2,1)S(1)}, bf16[1536,768]{1,0:T(8,128)(2,1)}, u32[]{:S(2)}) copy-start(bf16[1536,768]{1,0:T(8,128)(2,1)} %param.11) | copy-start | bytes 7077892
  7.2 25.2 %all-to-all-start = ((bf16[8,56,768]{2,1,0:T(8,128)(2,1)}), bf16[8,56,768]{2,1,0:T(8,128)(2,1)S(1)}, u32[]{:S(2)}, u32[]{:S(2)}) async-start(bf16[8,56,768]{2,1,0:T(8,128)(2,1)} %fusion.25), calls=%async_computation | async-start | bytes 1376256 | tf_op jit(solution)/shard_map/all_to_all | solution.py:54
  56.4 10.5 %copy-start.1 = (f32[1,3072]{1,0:T(1,128)S(1)}, f32[1,3072]{1,0:T(1,128)}, u32[]{:S(2)}) copy-start(f32[1,3072]{1,0:T(1,128)} %param.10) | copy-start | bytes 36868
  57.8 9.0 %all-to-all-start.2 = ((bf16[4,56,768]{2,1,0:T(8,128)(2,1)}), bf16[4,56,768]{2,1,0:T(8,128)(2,1)S(1)}, u32[]{:S(2)}, u32[]{:S(2)}) async-start(bf16[4,56,768]{2,1,0:T(8,128)(2,1)} %bitcast.22), calls=%async_computation.2 | async-start | bytes 688128 | tf_op jit(solution)/shard_map/all_to_all | solution.py:76
